TPU v7x, 256 devices: a whole 4x4x8 slice. The times are simulated.
256 devices in a mesh: tile: 32 (over z_lo, y, core), img: 8 (over x, z_hi).
Axes of the slice: x: 4, y: 4, z: 8 (z_hi: 2, z_lo: 4; z = z_hi * 4 + z_lo), core: 2. Of those that a mesh axis runs over, the one named last changes fastest.
Arguments:
- tower: bfloat16 [8, 64, 128, 256], P('img', 'tile'), may hold values from -6 to 6
- cls_weight: bfloat16 [720, 2304], replicated, may hold values from -0.125 to 0.125
- cls_bias: float32 [720], replicated, may hold values from -5.5 to -3.5
- box_weight: bfloat16 [36, 2304], replicated, may hold values from -0.125 to 0.125
- box_bias: float32 [36], replicated, may hold values from -0.5 to 0.5
- labels: int32 [8, 9, 64, 128], P('img', None, 'tile'), may hold values from -2 to 79, as said below
- target_index: int32 [8, 9, 64, 128], P('img', None, 'tile'), may hold values from 0 to 99
- boxes: float32 [8, 4, 100], P('img'), may hold values from -320 to 1344, as said below
Outputs:
- loss: float32 [], replicated
- cls_weight_grad: float32 [720, 2304], replicated
- cls_bias_grad: float32 [720], replicated
- box_weight_grad: float32 [36, 2304], replicated
- box_bias_grad: float32 [36], replicated
- tower_grad: bfloat16 [8, 64, 128, 256], P('img', 'tile')
Inputs may be any that keep to these rules, and one draw needn't show every extreme that they name: `labels`: -1 marks background and -2 an ignored anchor, other values are classes; every image has at least one anchor with a class. `boxes`: x1 < x2 and y1 < y2 in every box; sides between 8 and 640 pixels.
All inputs are finite; a program needn't handle non-finite values.
Results may differ from a plain program's by a relative error of at most 0.0053.
Values may be sent and summed in bfloat16 or wider, within the bound.
A program may use at most 64 MiB of HBM per device.

v0:
```python
import jax
import jax.numpy as jnp
from jax import lax
from jax.sharding import PartitionSpec as P

CLASSES = 80
ANCHORS = 9
STRIDE = 8
FOCAL_ALPHA = 0.25
NORM_EPS = 1e-06


def padded_2(value, sides, width):
    for axis, dim in sides:
        peers, length = (lax.axis_size(axis), value.shape[dim])
        up = [(i, (i + 1) % peers) for i in range(peers - 1)]
        down = [(j, i) for i, j in up]
        last = lax.slice_in_dim(value, length - width, length, axis=dim)
        initial = lax.slice_in_dim(value, 0, width, axis=dim)
        before = lax.ppermute(last, axis, up)
        after = lax.ppermute(initial, axis, down)
        value = jnp.concatenate([before, value, after], axis=dim)
    return value


def packed_total(arrays, axis):
    vector, at, gathered = (jnp.concatenate([a.reshape(-1) for a in arrays]), 0, [])
    subtotal = lax.psum(vector, axis)
    for a in arrays:
        gathered.append(subtotal[at : at + a.size].reshape(a.shape))
        at += a.size
    return tuple(gathered)


def build_patches(extended):
    rows_here = extended.shape[1] - 2
    columns = extended.shape[2]
    padded = jnp.pad(extended, ((0, 0), (0, 0), (1, 1), (0, 0)))
    pieces = []
    for row_tap in range(3):
        for col_tap in range(3):
            pieces.append(padded[:, row_tap : row_tap + rows_here, col_tap : col_tap + columns, :])
    return jnp.concatenate(pieces, axis=3)


def taps_back(dpatch, rows_lo, rows_out):
    images_here, rows_in, columns, width_all = dpatch.shape
    channels = width_all // 9
    pieces = dpatch.reshape(images_here, rows_in, columns, 9, channels)
    accumulated = jnp.zeros((images_here, rows_in + 2, columns + 2, channels), jnp.float32)
    for row_tap in range(3):
        for col_tap in range(3):
            accumulated = accumulated.at[
                :, row_tap : row_tap + rows_in, col_tap : col_tap + columns, :
            ].add(pieces[:, :, :, row_tap * 3 + col_tap, :])
    return accumulated[:, rows_lo : rows_lo + rows_out, 1 : columns + 1, :]


def head_terms(logits, deltas, labels, target_index, boxes, first_row):
    images_here = labels.shape[0]
    rows_here = labels.shape[2]
    columns = labels.shape[3]
    scores = logits.reshape(ANCHORS, CLASSES, images_here, rows_here, columns)
    assigned = jnp.transpose(labels, (1, 0, 2, 3))
    classes = lax.broadcasted_iota(jnp.int32, (1, CLASSES, 1, 1, 1), 1)
    target = (assigned[:, None] == classes).astype(jnp.float32)
    counted = (assigned >= -1).astype(jnp.float32)[:, None]
    probability = jax.nn.sigmoid(scores)
    hit_term = -FOCAL_ALPHA * (1.0 - probability) * (1.0 - probability) * jax.nn.log_sigmoid(scores)
    miss_term = -(1.0 - FOCAL_ALPHA) * probability * probability * jax.nn.log_sigmoid(-scores)
    focal_sum = jnp.sum(counted * (target * hit_term + (1.0 - target) * miss_term))
    offsets = deltas.reshape(ANCHORS, 4, images_here, rows_here, columns)
    anchor_ids = lax.broadcasted_iota(jnp.int32, (ANCHORS, 1, 1, 1), 0)
    scale_step = (anchor_ids // 3).astype(jnp.float32)
    ratio_step = (anchor_ids % 3 - 1).astype(jnp.float32)
    anchor_base = 4.0 * STRIDE * jnp.exp2(scale_step / 3.0)
    anchor_w = anchor_base * jnp.exp2(-ratio_step / 2.0)
    anchor_h = anchor_base * jnp.exp2(ratio_step / 2.0)
    row_ids = first_row + lax.broadcasted_iota(jnp.int32, (1, 1, rows_here, 1), 2)
    col_ids = lax.broadcasted_iota(jnp.int32, (1, 1, 1, columns), 3)
    centre_y = (row_ids.astype(jnp.float32) + 0.5) * STRIDE
    centre_x = (col_ids.astype(jnp.float32) + 0.5) * STRIDE
    middle_x = centre_x + offsets[:, 0] * anchor_w
    middle_y = centre_y + offsets[:, 1] * anchor_h
    pred_width = anchor_w * jnp.exp(offsets[:, 2])
    pred_height = anchor_h * jnp.exp(offsets[:, 3])
    pred_left = middle_x - 0.5 * pred_width
    pred_right = middle_x + 0.5 * pred_width
    pred_top = middle_y - 0.5 * pred_height
    pred_bottom = middle_y + 0.5 * pred_height
    flat_index = target_index.reshape(images_here, -1)
    picked = jnp.take_along_axis(
        boxes,
        jnp.broadcast_to(flat_index[:, None, :], (images_here, 4, flat_index.shape[1])),
        axis=2,
    )
    picked = jnp.transpose(
        picked.reshape(images_here, 4, ANCHORS, rows_here, columns), (1, 2, 0, 3, 4)
    )
    true_left, true_top, true_right, true_bottom = (picked[0], picked[1], picked[2], picked[3])
    crossing_w = jnp.maximum(
        jnp.minimum(pred_right, true_right) - jnp.maximum(pred_left, true_left), 0.0
    )
    crossing_h = jnp.maximum(
        jnp.minimum(pred_bottom, true_bottom) - jnp.maximum(pred_top, true_top), 0.0
    )
    crossing = crossing_w * crossing_h
    union_area = (
        pred_width * pred_height + (true_right - true_left) * (true_bottom - true_top) - crossing
    )
    outer_w = jnp.maximum(pred_right, true_right) - jnp.minimum(pred_left, true_left)
    outer_h = jnp.maximum(pred_bottom, true_bottom) - jnp.minimum(pred_top, true_top)
    outer_area = outer_w * outer_h
    giou_value = crossing / union_area - (outer_area - union_area) / outer_area
    positive = (assigned >= 0).astype(jnp.float32)
    giou_sum = jnp.sum(positive * (1.0 - giou_value))
    return (focal_sum, giou_sum)


def per_device(tower, cls_weight, cls_bias, box_weight, box_bias, labels, target_index, boxes):
    images_here = tower.shape[0]
    rows_here = tower.shape[1]
    columns = tower.shape[2]
    split_at = cls_weight.shape[0]
    weight_all = jnp.concatenate([cls_weight, box_weight], axis=0)
    bias_all = jnp.concatenate([cls_bias, box_bias])
    extended = padded_2(tower, (("tile", 1),), 1)
    patches = build_patches(extended)
    flat_patches = patches.reshape(-1, patches.shape[3])
    outputs = lax.dot_general(
        weight_all, flat_patches, (((1,), (1,)), ((), ())), preferred_element_type=jnp.float32
    )
    outputs = (outputs + bias_all[:, None]).reshape(
        weight_all.shape[0], images_here, rows_here, columns
    )
    first_row = lax.axis_index("tile") * rows_here

    def loss_pair(scores, offsets):
        return head_terms(scores, offsets, labels, target_index, boxes, first_row)

    loss_terms, pullback = jax.vjp(loss_pair, outputs[:split_at], outputs[split_at:])
    grad_scores, grad_offsets = pullback((jnp.ones((), jnp.float32), jnp.ones((), jnp.float32)))
    focal_local, giou_local = loss_terms
    count_local = jnp.sum((labels >= 0).astype(jnp.float32))
    grad_out = jnp.concatenate([grad_scores, grad_offsets], axis=0)
    grad_low = grad_out.astype(jnp.bfloat16)
    grad_flat = grad_low.reshape(grad_low.shape[0], -1)
    weight_terms = jnp.dot(grad_flat, flat_patches, preferred_element_type=jnp.float32)
    bias_terms = jnp.sum(grad_out, axis=(1, 2, 3))
    grad_rows = padded_2(grad_low, (("tile", 2),), 1)
    dpatch = lax.dot_general(
        grad_rows.reshape(grad_rows.shape[0], -1),
        weight_all,
        (((0,), (0,)), ((), ())),
        preferred_element_type=jnp.float32,
    )
    dpatch = dpatch.reshape(images_here, rows_here + 2, columns, weight_all.shape[1])
    tower_sum = taps_back(dpatch, 2, rows_here)
    tower_grad = tower_sum.astype(jnp.bfloat16)
    entries = weight_all.shape[0] * (weight_all.shape[1] + 1)
    focal_total, giou_total, positives, bias_sum = packed_total(
        (focal_local, giou_local, count_local, bias_terms), ("tile", "img")
    )
    weight_sum = lax.psum(weight_terms, ("tile", "img"))
    squares = jnp.sum(weight_sum * weight_sum) + jnp.sum(bias_sum * bias_sum)
    scale = lax.rsqrt(squares / entries + NORM_EPS)
    weight_norm = weight_sum * scale
    bias_norm = bias_sum * scale
    loss = (focal_total + giou_total) / positives
    return (
        loss,
        weight_norm[:split_at],
        bias_norm[:split_at],
        weight_norm[split_at:],
        bias_norm[split_at:],
        tower_grad,
    )


def solution(mesh):
    placed = (
        P("img", "tile", None, None),
        P(),
        P(),
        P(),
        P(),
        P("img", None, "tile", None),
        P("img", None, "tile", None),
        P("img", None, None),
    )
    return jax.shard_map(
        per_device,
        mesh=mesh,
        in_specs=placed,
        out_specs=(P(), P(), P(), P(), P(), P("img", "tile", None, None)),
        check_vma=False,
    )
```

profile of v0, /device:TPU:2, one launch (start us, length us, event | category | flops | bytes accessed | tf_op | source)
XLA Modules:
  0.0 431.4 jit_solution(16412508561127130968)
XLA Ops:
  7.2 1.5 fusion.90
  8.8 2.4 collective-permute-start
  11.1 1.3 collective-permute-start.1
  12.4 0.6 add_multiply_fusion.3
  13.0 0.5 exponential_multiply_fusion
  13.5 0.7 broadcast_in_dim.30
  14.3 0.6 fusion.94
  14.9 0.6 fusion.93
  15.6 1.3 compare_convert_fusion
  16.9 75.0 %gather_fusion = f32[9216]{0:T(1024)S(1)} fusion(f32[4,100]{1,0:T(4,128)S(1)} %bitcast.249, s32[9216]{0:T(1024)S(1)} %reshape.1606), kind=kCustom, calls=%fused_computation | custom fusion | bytes 147456 | tf_op jit(solution)/shard_map/jvp(jit(take_along_axis))/gather | solution.py:92
  92.0 2.2 constant_dynamic-update-slice_fusion.1
  94.3 3.6 copy.38
  97.8 1.4 and_reduce_fusion
  99.2 0.8 pad_maximum_fusion.3
  100.0 0.5 add_multiply_fusion.2
  100.5 1.0 fusion.43
  101.6 0.9 fusion.45
  102.5 0.9 constant_dynamic-update-slice_fusion.2
  103.5 0.9 fusion.44
  104.5 1.1 convolution_add_fusion
  105.8 0.4 reshape.1582
  106.1 0.8 minimum_subtract_fusion.1
  106.9 1.5 fusion.65
  108.4 0.9 multiply_multiply_fusion.5
  109.3 0.8 multiply_multiply_fusion.4
  110.1 0.1 add_multiply_fusion
  110.2 0.1 copy.34
  110.4 10.4 %fusion.82 = (bf16[9,80,1,2,128]{4,3,1,0,2:T(2,128)(2,1)S(1)}, f32[9,80,1,2,128]{4,3,1,0,2:T(2,128)}, f32[]{:T(128)}) fusion(f32[9,80,1,2,128]{4,3,1,0,2:T(2,128)S(1)} %reshape.1582, f32[9,2,128]{2,1,0:T(2,128)S(1)} %copy-done.7, s32[9,2,128]{2,1,0:T(2,128)S(1)} %bitcast.269), kind=kLoop, calls=%fused_computation.207 | loop fusion | flops 12718079 | bytes 1861636 | tf_op jit(solution)/shard_map/convert.4
  120.8 1.4 copy.33
  122.2 4.0 convolution_bitcast_fusion
  126.3 0.1 fusion.24
  126.4 3.8 collective-permute-start.2
  130.2 1.3 collective-permute-start.3
  131.5 0.1 fusion.25
  131.6 0.6 convert_reduce_fusion
  132.2 2.0 pad_maximum_fusion.4
  134.3 83.6 %psum.14 = f32[759]{0:T(1024)S(1)} all-reduce(f32[759]{0:T(1024)S(1)} %pad_maximum_fusion.4), channel_id=1, replica_groups=mesh['tile'=32,'img'=8] {'tile','img'}, use_global_device_ids=true, to_apply=%region_4.6 | all-reduce | flops 759 | bytes 6072 | tf_op jit(solution)/shard_map/psum | solution.py:28
  217.9 0.6 fusion.92
  220.4 0.7 multiply_reduce_fusion.2
  221.1 4.1 convolution_bitcast_fusion.1
  225.2 0.1 scatter-add.30
  225.3 2.1 copy-done.1
  227.4 1.3 fusion.35
  228.7 2.6 scatter-add.31
  231.3 3.0 add_select_fusion
  234.4 2.7 scatter-add.34
  237.1 1.2 fusion.34
  238.2 1.1 fusion.32
  239.4 1.4 scatter-add.36
  240.8 1.1 fusion.31
  241.9 1.4 scatter-add.39
  243.4 1.2 fusion.30
  244.5 1.1 fusion.28
  245.7 1.4 scatter-add.41
  247.1 1.1 fusion.27
  248.2 1.4 scatter-add.44
  249.7 0.7 slice.628
  250.4 158.2 %all-reduce.8.cloned.1.call-done = f32[756,2304]{1,0:T(8,128)} async-done(((f32[756,2304]{1,0:T(8,128)}), f32[756,2304]{1,0:T(8,128)}) %all-reduce.8.cloned.1.call-update) | async-done | bytes 6967312 | tf_op jit(solution)/shard_map/psum | solution.py:164
  408.5 5.4 %multiply_reduce_fusion = f32[]{:T(128)} fusion(f32[756,2304]{1,0:T(8,128)} %all-reduce.8.cloned.1.call-done), kind=kLoop, calls=%fused_computation.1 | loop fusion | flops 3483647 | bytes 6967300 | tf_op jit(solution)/shard_map/reduce_sum | solution.py:165
  415.3 0.1 slice_multiply_fusion
  415.3 3.4 broadcast_multiply_fusion
  418.8 0.8 slice.511
  419.6 3.2 slice.510
  422.8 0.6 slice.469
  (51 shorter events, 0.7 us)
Async XLA Ops:
  7.2 9.8 %copy-start = (f32[1,4,100]{2,1,0:T(4,128)S(1)}, f32[1,4,100]{2,1,0:T(4,128)}, u32[]{:S(2)}) copy-start(f32[1,4,100]{2,1,0:T(4,128)} %param.34) | copy-start | bytes 4804
  7.2 401.4 %all-reduce.8.cloned.1.call-start = ((), (), s32[]{:S(2)}) async-start(), calls=%async_computation | async-start | bytes 14008320 | tf_op jit(solution)/shard_map/psum | solution.py:164
  8.8 91.8 %collective-permute-start = (bf16[1,1,128,256]{3,2,1,0:T(8,128)(2,1)}, bf16[1,1,128,256]{3,2,1,0:T(8,128)(2,1)}, u32[]{:S(2)}, u32[]{:S(2)}) collective-permute-start(bf16[1,1,128,256]{3,2,1,0:T(8,128)(2,1)} %get-tuple-element.146), channel_id=1, source_target_pairs={{0,8},{8,16},{16,24},{24,32},{32,40},{40,48},{48,56},{56,64},{64,7... | collective-permute-start | bytes 196616 | tf_op jit(solution)/shard_map/ppermute | solution.py:20
  11.1 89.4 %collective-permute-start.1 = (bf16[1,1,128,256]{3,2,1,0:T(8,128)(2,1)}, bf16[1,1,128,256]{3,2,1,0:T(8,128)(2,1)}, u32[]{:S(2)}, u32[]{:S(2)}) collective-permute-start(bf16[1,1,128,256]{3,2,1,0:T(8,128)(2,1)} %get-tuple-element.147), channel_id=1, source_target_pairs={{8,0},{16,8},{24,16},{32,24},{40,32},{48,40},{56,48},{64,56},{72,6... | collective-permute-start | bytes 196616 | tf_op jit(solution)/shard_map/ppermute | solution.py:21
  13.0 3.9 copy-start.8
  92.0 2.3 copy-start.4
  104.4 1.2 copy-start.2
  105.6 4.4 %copy-start.6 = (f32[9]{0:T(128)S(1)}, f32[9]{0:T(128)}, u32[]{:S(2)}) copy-start(f32[9]{0:T(128)} %get-tuple-element.161) | copy-start | bytes 112
  105.6 4.7 %copy-start.5 = (s32[1,9,2,128]{3,2,1,0:T(2,128)S(1)}, s32[1,9,2,128]{3,2,1,0:T(2,128)}, u32[]{:S(2)}) copy-start(s32[1,9,2,128]{3,2,1,0:T(2,128)} %param.32) | copy-start | bytes 27652
  105.6 4.7 %copy-start.7 = (f32[9,2,128]{2,1,0:T(2,128)S(1)}, f32[9,2,128]{2,1,0:T(2,128)}, u32[]{:S(2)}) copy-start(f32[9,2,128]{2,1,0:T(2,128)} %compare_convert_fusion) | copy-start | bytes 27652
  105.7 16.5 %copy-start.3 = (bf16[1,2,128,2304]{3,2,1,0:T(8,128)(2,1)S(1)}, bf16[1,2,128,2304]{3,2,1,0:T(8,128)(2,1)}, u32[]{:S(2)}) copy-start(bf16[1,2,128,2304]{3,2,1,0:T(8,128)(2,1)} %copy-done.2) | copy-start | bytes 3538948
  126.4 94.7 %collective-permute-start.2 = (bf16[756,1,1,128]{0,3,2,1:T(8,128)(2,1)S(1)}, bf16[756,1,1,128]{0,3,2,1:T(8,128)(2,1)S(1)}, u32[]{:S(2)}, u32[]{:S(2)}) collective-permute-start(bf16[756,1,1,128]{0,3,2,1:T(8,128)(2,1)S(1)} %get-tuple-element.144), channel_id=1, source_target_pairs={{0,8},{8,16},{16,24},{24,32},{32,40},{40,48},{48,56},{56,64},{64,7... | collective-permute-start | bytes 580616 | tf_op jit(solution)/shard_map/ppermute | solution.py:20
  130.2 90.9 %collective-permute-start.3 = (bf16[756,1,1,128]{0,3,2,1:T(8,128)(2,1)S(1)}, bf16[756,1,1,128]{0,3,2,1:T(8,128)(2,1)S(1)}, u32[]{:S(2)}, u32[]{:S(2)}) collective-permute-start(bf16[756,1,1,128]{0,3,2,1:T(8,128)(2,1)S(1)} %get-tuple-element.145), channel_id=1, source_target_pairs={{8,0},{16,8},{24,16},{32,24},{40,32},{48,40},{56,48},{64,56},{72,6... | collective-permute-start | bytes 580616 | tf_op jit(solution)/shard_map/ppermute | solution.py:21
  225.2 2.2 copy-start.1
  415.3 7.5 %copy-start.9 = (f32[756]{0:T(1024)}, f32[756]{0:T(1024)S(1)}, u32[]{:S(2)}) copy-start(f32[756]{0:T(1024)S(1)} %slice_multiply_fusion) | copy-start | bytes 9076
Sparse Core Ops, SparseCore 0:
  126.4 282.1 all-reduce.7
where the time goes:
time: 433 us; the launch traced here: 431 us
  waiting for transfers between devices  158 us (36%)
  local copies, waits for them, and re-layouts  107 us (25%)
  blocking collectives  83.6 us (19%)
  other arithmetic  46 us (11%)
  between operations  19 us (4%)
  matrix products  9.24 us (2%)
  starting transfers between devices  8.76 us (2%)
    psum x1, waiting for transfers between devices, per_device(): weight_sum = lax.psum(weight_terms, ('tile', 'img'))  158 us
    psum x1, blocking collectives, packed_total(): subtotal = lax.psum(vector, axis)  83.6 us
    gather x3, local copies, waits for them, and re-layouts, head_terms(): jnp.take_along_axis(boxes, jnp.broadcast_to(flat_index[:, None, :], (imag...  75 us
    another operation x5, other arithmetic  14.9 us
    scatter-add x7, local copies, waits for them, and re-layouts, taps_back(): accumulated = accumulated.at[:, row_tap:row_tap + rows_in, col_tap:col_ta...  11.1 us
  transfers between devices with their start and end apart: 5, of which 1 were waited for; matrix products, arithmetic and copies ran while one was open for 28% of the time, Pallas kernels for 0%

commit v1 on v0

--- a/solution.py
+++ b/solution.py
@@ -25,7 +25,13 @@
 
 def packed_total(arrays, axis):
     vector, at, gathered = (jnp.concatenate([a.reshape(-1) for a in arrays]), 0, [])
-    subtotal = lax.psum(vector, axis)
+
+    def bands_hold(local_block):
+        tmp = jax.lax.all_gather(local_block, axis_name=axis)
+        work_now = jnp.sum(tmp, 0)
+        return work_now
+
+    subtotal = bands_hold(vector)
     for a in arrays:
         gathered.append(subtotal[at : at + a.size].reshape(a.shape))
         at += a.size

time: 433 us -> 452 us (1.044)
  waiting for transfers between devices: 158 us -> 243 us
  blocking collectives: 83.6 us -> 0 us
  local copies, waits for them, and re-layouts: 107 us -> 119 us
  other arithmetic: 46 us -> 50.6 us
    unnamed x1 -> x2, waiting for transfers between devices: 0.02 us -> 241 us
    psum x1 -> x0, waiting for transfers between devices: 158 us -> none  [per_device(): weight_sum = lax.psum(weight_terms, ('tile', 'img'))]
    psum x1 -> x0, blocking collectives: 83.6 us -> none  [packed_total(): subtotal = lax.psum(vector, axis)]
  transfers between devices with their start and end apart: 5 -> 5, of which waited for: 1 -> 2; matrix products, arithmetic and copies ran while one was open for 28% -> 26% of each run, Pallas kernels for 0% -> 0%
where the time goes in v1:
time: 452 us; the launch traced here: 450 us
  waiting for transfers between devices  243 us (54%)
  local copies, waits for them, and re-layouts  119 us (26%)
  other arithmetic  50.6 us (11%)
  between operations  18.8 us (4%)
  matrix products  10.5 us (2%)
  starting transfers between devices  8.94 us (2%)
    unnamed x2, waiting for transfers between devices  241 us
    gather x3, local copies, waits for them, and re-layouts, head_terms(): jnp.take_along_axis(boxes, jnp.broadcast_to(flat_index[:, None, :], (imag...  75 us
    another operation x5, other arithmetic  15.2 us
    scatter-add x7, local copies, waits for them, and re-layouts, taps_back(): accumulated = accumulated.at[:, row_tap:row_tap + rows_in, col_tap:col_ta...  11.2 us
  transfers between devices with their start and end apart: 5, of which 2 were waited for; matrix products, arithmetic and copies ran while one was open for 26% of the time, Pallas kernels for 0%

profile of v1, /device:TPU:2, one launch (start us, length us, event | category | flops | bytes accessed | tf_op | source)
XLA Modules:
  0.0 450.4 jit_solution(7481260401381997833)
XLA Ops:
  7.2 1.5 fusion.90
  8.8 2.4 collective-permute-start
  11.1 1.3 collective-permute-start.1
  13.5 0.7 broadcast_in_dim.30
  14.2 1.3 compare_convert_fusion
  15.6 75.0 %gather_fusion = f32[9216]{0:T(1024)S(1)} fusion(f32[4,100]{1,0:T(4,128)S(1)} %bitcast.249, s32[9216]{0:T(1024)S(1)} %reshape.1606), kind=kCustom, calls=%fused_computation | custom fusion | bytes 147456 | tf_op jit(solution)/shard_map/jvp(jit(take_along_axis))/gather | solution.py:98
  90.7 0.6 fusion.91
  91.3 2.2 constant_dynamic-update-slice_fusion.1
  93.5 0.9 constant_dynamic-update-slice_fusion
  95.0 1.0 fusion.43
  96.0 0.9 fusion.45
  97.0 0.9 constant_dynamic-update-slice_fusion.2
  98.0 0.9 fusion.44
  98.9 1.0 copy-done.2
  99.9 1.1 convolution_add_fusion
  101.1 0.6 slice.501
  101.7 0.9 slice.500
  102.6 0.8 reshape.1584
  103.4 2.4 reshape.1582
  105.8 1.6 fusion.65
  107.4 0.7 convert_reduce_fusion
  108.1 0.8 minimum_subtract_fusion.1
  108.9 1.0 multiply_multiply_fusion.5
  109.8 0.8 multiply_multiply_fusion.4
  110.7 0.7 add_multiply_fusion
  112.1 0.8 copy.34
  112.8 11.4 %fusion.82 = (bf16[9,80,1,2,128]{4,3,1,0,2:T(2,128)(2,1)S(1)}, f32[9,80,1,2,128]{4,3,1,0,2:T(2,128)}, f32[]{:T(128)}) fusion(f32[9,80,1,2,128]{4,3,1,0,2:T(2,128)} %reshape.1582, f32[9,2,128]{2,1,0:T(2,128)} %compare_convert_fusion, s32[9,2,128]{2,1,0:T(2,128)} %bitcast.269), kind=kLoop, calls=%fused_computation.207 | loop fusion | flops 12718079 | bytes 1861636 | tf_op jit(solution)/shard_map/convert.4
  124.2 0.8 copy.35
  125.0 2.1 copy.33
  127.1 1.3 fusion.25
  128.4 5.4 %convolution_bitcast_fusion = f32[756,2304]{1,0:T(8,128)} fusion(bf16[1,2,128,2304]{3,2,1,0:T(8,128)(2,1)} %copy-done.2, bf16[36,2,128]{2,0,1:T(8,128)(2,1)S(1)} %copy-done.3, bf16[720,2,128]{2,0,1:T(8,128)(2,1)} %bitcast.252), kind=kOutput, calls=%fused_computation.2 | convolution fusion | flops 892588032 | bytes 8534016 | tf_op jit(solution)/shard_map/dot_general | solution.py:154
  133.8 0.9 broadcast.1191
  134.8 3.4 maximum_dynamic-update-slice_fusion
  138.2 3.6 copy.38
  142.4 1.3 fusion.24
  143.7 3.8 collective-permute-start.2
  147.5 1.5 collective-permute-start.3
  149.6 0.7 and_reduce_fusion
  150.3 1.8 collective-permute-done.3
  152.1 4.0 convolution_bitcast_fusion.1
  156.3 2.1 copy-done.1
  158.3 1.4 fusion.35
  159.7 2.7 scatter-add.31
  162.4 3.1 add_select_fusion
  165.5 2.7 scatter-add.34
  168.3 1.2 fusion.34
  169.4 1.1 fusion.32
  170.6 1.4 scatter-add.36
  172.0 1.2 fusion.31
  173.2 1.4 scatter-add.39
  174.6 1.2 fusion.30
  175.8 1.1 fusion.28
  176.9 1.4 scatter-add.41
  178.3 1.1 fusion.27
  179.5 1.4 scatter-add.44
  180.9 0.7 slice.628
  181.6 240.8 %all-reduce.10.cloned.1.call-done = (f32[194304]{0:T(1024)}, f32[756,2304]{1,0:T(8,128)}) async-done(((f32[194304]{0:T(1024)}, f32[756,2304]{1,0:T(8,128)}), (f32[194304]{0:T(1024)}, f32[756,2304]{1,0:T(8,128)})) %all-reduce.10.cloned.1.call-update) | async-done | bytes 7744528
  422.4 1.9 reshape.1612
  424.3 0.7 multiply_reduce_fusion.2
  425.0 0.6 fusion.92
  425.6 5.4 %multiply_reduce_fusion = f32[]{:T(128)} fusion(f32[756,2304]{1,0:T(8,128)} %get-tuple-element.123), kind=kLoop, calls=%fused_computation.1 | loop fusion | flops 3483647 | bytes 6967300 | tf_op jit(solution)/shard_map/reduce_sum | solution.py:171
  432.4 3.4 broadcast_multiply_fusion
  435.9 0.8 slice.511
  436.6 3.2 slice.510
  (49 shorter events, 4.7 us)
Async XLA Ops:
  7.2 8.4 %copy-start = (f32[1,4,100]{2,1,0:T(4,128)S(1)}, f32[1,4,100]{2,1,0:T(4,128)}, u32[]{:S(2)}) copy-start(f32[1,4,100]{2,1,0:T(4,128)} %param.34) | copy-start | bytes 4804
  7.2 415.2 %all-reduce.10.cloned.1.call-start = ((), (), s32[]{:S(2)}) async-start(), calls=%async_computation | async-start | bytes 15564800
  8.8 86.2 %collective-permute-start = (bf16[1,1,128,256]{3,2,1,0:T(8,128)(2,1)}, bf16[1,1,128,256]{3,2,1,0:T(8,128)(2,1)}, u32[]{:S(2)}, u32[]{:S(2)}) collective-permute-start(bf16[1,1,128,256]{3,2,1,0:T(8,128)(2,1)} %get-tuple-element.148), channel_id=1, source_target_pairs={{0,8},{8,16},{16,24},{24,32},{32,40},{40,48},{48,56},{56,64},{64,7... | collective-permute-start | bytes 196616 | tf_op jit(solution)/shard_map/ppermute | solution.py:20
  11.1 83.9 %collective-permute-start.1 = (bf16[1,1,128,256]{3,2,1,0:T(8,128)(2,1)}, bf16[1,1,128,256]{3,2,1,0:T(8,128)(2,1)}, u32[]{:S(2)}, u32[]{:S(2)}) collective-permute-start(bf16[1,1,128,256]{3,2,1,0:T(8,128)(2,1)} %get-tuple-element.149), channel_id=1, source_target_pairs={{8,0},{16,8},{24,16},{32,24},{40,32},{48,40},{56,48},{64,56},{72,6... | collective-permute-start | bytes 196616 | tf_op jit(solution)/shard_map/ppermute | solution.py:21
  90.6 2.9 copy-start.4
  90.6 2.9 copy-start.6
  98.9 1.0 copy-start.2
  112.8 15.6 %copy-start.3 = (bf16[36,2,128]{2,0,1:T(8,128)(2,1)S(1)}, bf16[36,2,128]{2,0,1:T(8,128)(2,1)}, u32[]{:S(2)}) copy-start(bf16[36,2,128]{2,0,1:T(8,128)(2,1)} %copy.37) | copy-start | bytes 55300
  138.2 11.4 %copy-start.7 = (s32[4]{0:T(128)S(1)}, s32[4]{0:T(128)}, u32[]{:S(2)}) copy-start(s32[4]{0:T(128)} %constant.358.clone.1) | copy-start | bytes 52
  143.7 6.6 %collective-permute-start.2 = (bf16[756,1,1,128]{0,3,2,1:T(8,128)(2,1)S(1)}, bf16[756,1,1,128]{0,3,2,1:T(8,128)(2,1)S(1)}, u32[]{:S(2)}, u32[]{:S(2)}) collective-permute-start(bf16[756,1,1,128]{0,3,2,1:T(8,128)(2,1)S(1)} %get-tuple-element.146), channel_id=1, source_target_pairs={{0,8},{8,16},{16,24},{24,32},{32,40},{40,48},{48,56},{56,64},{64,7... | collective-permute-start | bytes 580616 | tf_op jit(solution)/shard_map/ppermute | solution.py:20
  147.5 4.6 %collective-permute-start.3 = (bf16[756,1,1,128]{0,3,2,1:T(8,128)(2,1)S(1)}, bf16[756,1,1,128]{0,3,2,1:T(8,128)(2,1)S(1)}, u32[]{:S(2)}, u32[]{:S(2)}) collective-permute-start(bf16[756,1,1,128]{0,3,2,1:T(8,128)(2,1)S(1)} %get-tuple-element.147), channel_id=1, source_target_pairs={{8,0},{16,8},{24,16},{32,24},{40,32},{48,40},{56,48},{64,56},{72,6... | collective-permute-start | bytes 580616 | tf_op jit(solution)/shard_map/ppermute | solution.py:21
  156.1 2.2 copy-start.1
  435.9 4.0 copy-start.5
Sparse Core Ops, SparseCore 0:
  138.3 284.0 all-reduce.9
